TPU v7x, 256 devices: a whole 4x4x8 slice. The times are simulated.
256 devices in a mesh: orb: 4 (over y), grid: 64 (over z, x, core).
Axes of the slice: x: 4, y: 4, z: 8, core: 2. Of those that a mesh axis runs over, the one named last changes fastest.
Arguments:
- orbitals: float32 [256, 2048, 128], P('orb', 'grid'), may hold values from -6 to 6
- previous: float32 [256, 2048, 128], P('orb', 'grid'), may hold values from -6 to 6
- potential: float32 [256, 2048, 128], P('orb', 'grid'), may hold values from -3 to 3
- partners: int32 [256, 3], P(('orb', 'grid')), may hold values from 0 to 255, as said below
- offsets: int32 [256, 3, 3], P(('orb', 'grid')), may hold values from -16 to 16, as said below
Outputs:
- advanced: float32 [256, 2048, 128], P('orb', 'grid')
- exchange_force: float32 [256, 2048, 128], P('orb', 'grid')
Inputs may be any that keep to these rules, and one draw needn't show every extreme that they name: `partners`: row n names three different orbitals among n + 1 to n + 4, counted modulo 256; so every intersecting pair is listed once, by its first orbital. There are integer box corners of the orbitals with offsets[n, q, :] = corner[partners[n, q]] - corner[n]; both ends of the range occur in every draw.
All inputs are finite; a program needn't handle non-finite values.
Results may differ from a plain program's by a relative error of at most 0.0003.
Values sent between devices are 32-bit elements; how exact they have to be, the bound alone decides.
No kernel may reach another device: no remote copies, remote signals or barrier semaphores. Data moves between devices by JAX's collectives and lax.ppermute only.
A program may use at most 128 MiB of HBM per device.

v0:
```python
import math
import jax
import jax.numpy as jnp
from jax import lax
from jax.sharding import Mesh
from jax.sharding import PartitionSpec as P

B = 64
SWEEPS = 4
AHEAD = 4
GRID = ("grid_0", "grid_1", "grid_2")
ORB_GRID = ("orb", "grid_0", "grid_1", "grid_2")
coulomb_factor = 4.0 * math.pi
exact_share = 0.25
verlet_factor = 0.05
lower_edge = 0.5
upper_edge = 16.0


def from_behind(array, axis, by):
    count = lax.axis_size(axis)
    return lax.ppermute(array, axis, [(i, (i + by) % count) for i in range(count)])


def cut_along(array, dim, count):
    before, after = (array.shape[:dim], array.shape[dim + 1 :])
    return jnp.moveaxis(array.reshape(*before, count, -1, *after), dim, 0)


def joined_along(blocks, dim):
    blocks = jnp.moveaxis(blocks, 0, dim)
    lengths = blocks.shape
    return blocks.reshape(*lengths[:dim], lengths[dim] * lengths[dim + 1], *lengths[dim + 2 :])


def exchange_in_order(blocks, axes, sequence):
    inside = blocks.shape[1:]
    out = blocks.reshape(*(lax.axis_size(a) for a in axes), *inside)
    for k in sequence:
        out = lax.all_to_all(out, axes[k], k, k, tiled=True)
    return out.reshape(-1, *inside)


def two_step_exchange(array, groups, sequence, split_dim, concat_dim):
    count = lax.axis_size(groups[0]) * lax.axis_size(groups[1])
    blocks = cut_along(array, split_dim, count)
    return joined_along(exchange_in_order(blocks, groups, sequence), concat_dim)


def apply_operator(grid_field):
    leading = grid_field.ndim - 3
    padded = jnp.pad(grid_field, [(0, 0)] * leading + [(2, 2)] * 3)
    extent = grid_field.shape[-1]

    def displaced(axis_number, offset_cells):
        corner = [2, 2, 2]
        corner[axis_number] = 2 + offset_cells
        return padded[
            ...,
            corner[0] : corner[0] + extent,
            corner[1] : corner[1] + extent,
            corner[2] : corner[2] + extent,
        ]

    nearest = (
        displaced(0, 1)
        + displaced(0, -1)
        + displaced(1, 1)
        + displaced(1, -1)
        + displaced(2, 1)
        + displaced(2, -1)
    )
    farther = (
        displaced(0, 2)
        + displaced(0, -2)
        + displaced(1, 2)
        + displaced(1, -2)
        + displaced(2, 2)
        + displaced(2, -2)
    )
    return 7.5 * grid_field - 4.0 / 3.0 * nearest + 1.0 / 12.0 * farther


def sweep_weights():
    centre = 0.5 * (upper_edge + lower_edge)
    radius = 0.5 * (upper_edge - lower_edge)
    ratio_sigma = centre / radius
    previous_rho = 1.0 / ratio_sigma
    weights = []
    for turn_index in range(SWEEPS - 1):
        current_rho = 1.0 / (2.0 * ratio_sigma - previous_rho)
        weights.append((current_rho * previous_rho, 2.0 * current_rho / radius))
        previous_rho = current_rho
    return (centre, weights)


def solve_potential(density):
    centre, weights = sweep_weights()
    residual = coulomb_factor * density
    direction = residual / centre
    solution = jnp.zeros_like(density)
    for turn_index in range(SWEEPS):
        solution = solution + direction
        residual = residual - apply_operator(direction)
        if turn_index + 1 < SWEEPS:
            keep_weight, residual_weight = weights[turn_index]
            direction = keep_weight * direction + residual_weight * residual
    return solution


def shift_box(one_box, offset, direction_sign):
    extent = one_box.shape[0]
    reach_cells = extent // 4
    padded = jnp.pad(one_box, reach_cells)
    corner = (reach_cells + direction_sign * offset).astype(jnp.int32)
    return lax.dynamic_slice(padded, (corner[0], corner[1], corner[2]), (extent, extent, extent))


def pair_terms(own_box, partner_boxes, pair_offsets):

    def single(partner_box, offset):
        moved_box = shift_box(partner_box, offset, 1)
        potential_box = solve_potential(own_box * moved_box)
        return (potential_box * moved_box, shift_box(potential_box * own_box, offset, -1))

    own_terms, partner_terms = jax.vmap(single)(partner_boxes, pair_offsets)
    return (jnp.sum(own_terms, axis=0), partner_terms)


def build_windows(orbitals, upper_rows, count_local, steps_ahead):
    slab_count = lax.axis_size(GRID)
    tail_shape = orbitals.shape[1:]
    blocks = jnp.concatenate([orbitals, upper_rows], axis=0)
    blocks = blocks.reshape((slab_count + steps_ahead, count_local) + tail_shape)
    ahead_rows = jnp.concatenate(
        [blocks[distance + 1 : distance + 1 + slab_count] for distance in range(steps_ahead)],
        axis=1,
    )
    windows = jnp.concatenate([blocks[:slab_count], ahead_rows], axis=1)
    return windows.reshape((slab_count * (count_local + AHEAD),) + tail_shape)


def fold_windows(returned, count_local, steps_ahead):
    slab_count = lax.axis_size(GRID)
    tail_shape = returned.shape[1:]
    blocks = returned.reshape((slab_count, count_local + AHEAD) + tail_shape)
    ahead_rows = blocks[:, count_local:]
    summed = jnp.pad(blocks[:, :count_local], ((0, steps_ahead), (0, 0), (0, 0), (0, 0)))
    for distance in range(steps_ahead):
        ahead_part = ahead_rows[:, distance * count_local : (distance + 1) * count_local]
        summed = summed + jnp.pad(
            ahead_part, ((distance + 1, steps_ahead - distance - 1), (0, 0), (0, 0), (0, 0))
        )
    flattened = summed.reshape(((slab_count + steps_ahead) * count_local,) + tail_shape)
    kept_rows = slab_count * count_local
    spilled = from_behind(flattened[kept_rows : kept_rows + AHEAD], "orb", 1)
    return flattened[:kept_rows] + jnp.pad(spilled, ((0, kept_rows - AHEAD), (0, 0), (0, 0)))


def local(orbitals, previous, potential, partners, offsets):
    count_local = partners.shape[0]
    width_last = orbitals.shape[2]
    total_orbitals = lax.axis_size(ORB_GRID) * count_local
    steps_ahead = -(-AHEAD // count_local)
    upper_rows = from_behind(orbitals[:AHEAD], "orb", -1)
    windows = build_windows(orbitals, upper_rows, count_local, steps_ahead)
    widened = lax.all_to_all(windows, GRID, split_axis=0, concat_axis=1, tiled=True)
    full_rows = widened.shape[1]
    extended = widened.reshape(count_local + AHEAD, B, B, B)
    own_boxes = extended[:count_local]
    first_index = lax.axis_index(ORB_GRID) * count_local
    local_index = jnp.remainder(partners - first_index, total_orbitals)

    def per_orbital(packed):
        own_box, chosen, pair_offsets = packed
        return pair_terms(own_box, extended[chosen], pair_offsets)

    own_force, partner_force = lax.map(per_orbital, (own_boxes, local_index, offsets))
    spread = (
        jnp.zeros_like(extended)
        .at[local_index.reshape(-1)]
        .add(partner_force.reshape((-1,) + extended.shape[1:]))
    )
    kinetic = (-0.5 * apply_operator(own_boxes)).reshape(count_local, full_rows, width_last)
    all_force = jnp.concatenate([own_force + spread[:count_local], spread[count_local:]], axis=0)
    packed_all = (exact_share * all_force).reshape(count_local + AHEAD, full_rows, width_last)
    returned, restored = (
        two_step_exchange(packed_all, (("grid_0", "grid_1"), "grid_2"), (0, 1), 1, 0),
        two_step_exchange(kinetic, (("grid_0", "grid_1"), "grid_2"), (0, 1), 1, 0),
    )
    exchange_force = fold_windows(returned, count_local, steps_ahead)
    advanced = (
        2.0 * orbitals
        - previous
        + verlet_factor * (restored + exchange_force - potential * orbitals)
    )
    return (advanced, exchange_force)


def solution(mesh):
    split = Mesh(
        mesh.devices.reshape(mesh.shape["orb"], 8, 4, 2), ("orb", "grid_0", "grid_1", "grid_2")
    )
    return jax.shard_map(
        local,
        mesh=split,
        in_specs=(
            P("orb", GRID, None),
            P("orb", GRID, None),
            P("orb", GRID, None),
            P(ORB_GRID, None),
            P(ORB_GRID, None, None),
        ),
        out_specs=(P("orb", GRID, None), P("orb", GRID, None)),
        check_vma=False,
    )
```

profile of v0, /device:TPU:2, one launch (start us, length us, event | category | flops | bytes accessed | tf_op | source)
XLA Modules:
  0.0 577.9 jit_solution(16364896627483350653)
XLA Ops:
  9.8 12.2 %all-to-all-start = ((f32[320,32,128]{2,1,0:T(8,128)}), f32[320,32,128]{2,1,0:T(8,128)}, u32[]{:S(2)}, u32[]{:S(2)}) async-start(f32[320,32,128]{2,1,0:T(8,128)} %bitcast.114), calls=%async_computation | async-start | bytes 10485760 | tf_op jit(solution)/shard_map/all_to_all | solution.py:167
  22.4 118.1 %all-to-all-done = f32[320,32,128]{2,1,0:T(8,128)} async-done(((f32[320,32,128]{2,1,0:T(8,128)}), f32[320,32,128]{2,1,0:T(8,128)}, u32[]{:S(2)}, u32[]{:S(2)}) %all-to-all-start) | async-done | bytes 5242912 | tf_op jit(solution)/shard_map/all_to_all | solution.py:167
  140.6 8.5 %reshape.78 = f32[5,64,64,64]{3,2,0,1:T(8,128)} reshape(f32[5,64,32,128]{3,2,0,1:T(8,128)} %bitcast.10) | data formatting | bytes 10485760 | tf_op jit(solution)/shard_map/reshape | solution.py:169
  152.4 7.5 %gather_fusion = f32[3,64,64,64]{3,2,1,0:T(8,128)} fusion(f32[5,64,64,64]{3,2,0,1:T(8,128)} %reshape.78, s32[1024]{0:T(1024)S(1)} %pad_clamp_fusion), kind=kCustom, calls=%fused_computation | custom fusion | bytes 6291468 | tf_op jit(solution)/shard_map/while/body/eval_jaxpr/gather | solution.py:176
  159.9 10.5 %pad.51 = f32[3,96,96,96]{3,2,1,0:T(8,128)} pad(f32[3,64,64,64]{3,2,1,0:T(8,128)} %gather_fusion, f32[]{:T(128)} %constant.49.clone.1), padding=0_0x16_16x16_16x16_16 | pad | bytes 13762564 | tf_op jit(solution)/shard_map/while/body/eval_jaxpr/vmap(jit(_pad))/pad | solution.py:114
  170.4 3.5 broadcast.154.clone
  173.9 20.5 %while.2 = (s32[]{:T(128)}, f32[3,96,96,96]{3,2,1,0:T(8,128)}, s32[3,4]{1,0:T(4,128)S(1)}, f32[3,64,64,64]{3,2,1,0:T(8,128)}, s32[]{:T(128)}) while((s32[]{:T(128)}, f32[3,96,96,96]{3,2,1,0:T(8,128)}, s32[3,4]{1,0:T(4,128)S(1)}, f32[3,64,64,64]{3,2,1,0:T(8,128)}, s32[]{:T(128)}) %tuple.70), condition=%wide.while_cond, body=%wide.while_body.sunk | while | flops 2 | bytes 4196993 | solution.py:116
  174.6 6.2 %dynamic-slice_dynamic-update-slice_fusion.4 = f32[3,64,64,64]{3,2,1,0:T(8,128)} fusion(f32[3,64,64,64]{3,2,1,0:T(8,128)} %get-tuple-element.203, s32[]{:T(128)} %get-tuple-element.200, f32[3,96,96,96]{3,2,1,0:T(8,128)} %get-tuple-element.206, s32[]{:T(128)} %bitcast.104, s32[]{:T(128)} %bitcast.105, s32[]{:T(128)} %bitcast.106, s32[]{:T(128)} %bitcast.107), kind=kLoop, calls=%fused_computation.2.clone.1 | loop fusion | bytes 4196864 | tf_op jit(solution)/shard_map/while/body/eval_jaxpr/vmap()/gather
  181.5 6.1 %dynamic-slice_dynamic-update-slice_fusion.4 = f32[3,64,64,64]{3,2,1,0:T(8,128)} fusion(f32[3,64,64,64]{3,2,1,0:T(8,128)} %get-tuple-element.203, s32[]{:T(128)} %get-tuple-element.200, f32[3,96,96,96]{3,2,1,0:T(8,128)} %get-tuple-element.206, s32[]{:T(128)} %bitcast.104, s32[]{:T(128)} %bitcast.105, s32[]{:T(128)} %bitcast.106, s32[]{:T(128)} %bitcast.107), kind=kLoop, calls=%fused_computation.2.clone.1 | loop fusion | bytes 4196864 | tf_op jit(solution)/shard_map/while/body/eval_jaxpr/vmap()/gather
  188.3 6.2 %dynamic-slice_dynamic-update-slice_fusion.4 = f32[3,64,64,64]{3,2,1,0:T(8,128)} fusion(f32[3,64,64,64]{3,2,1,0:T(8,128)} %get-tuple-element.203, s32[]{:T(128)} %get-tuple-element.200, f32[3,96,96,96]{3,2,1,0:T(8,128)} %get-tuple-element.206, s32[]{:T(128)} %bitcast.104, s32[]{:T(128)} %bitcast.105, s32[]{:T(128)} %bitcast.106, s32[]{:T(128)} %bitcast.107), kind=kLoop, calls=%fused_computation.2.clone.1 | loop fusion | bytes 4196864 | tf_op jit(solution)/shard_map/while/body/eval_jaxpr/vmap()/gather
  194.5 6.9 %multiply_multiply_fusion = f32[3,64,64,64]{3,2,1,0:T(8,128)} fusion(f32[3,64,64,64]{3,2,1,0:T(8,128)} %get-tuple-element.30, f32[64,64,64]{2,1,0:T(8,128)S(1)} %mul.171), kind=kLoop, calls=%fused_computation.93 | loop fusion | flops 1572864 | bytes 7340032 | tf_op jit(solution)/shard_map/while/body/eval_jaxpr/vmap()/div | solution.py:100
  201.3 35.3 %multiply_add_fusion.1 = (f32[3,64,64,64]{3,2,1,0:T(8,128)}, f32[3,64,64,64]{3,2,1,0:T(8,128)}) fusion(f32[3,64,64,64]{3,2,1,0:T(8,128)} %get-tuple-element.30, f32[64,64,64]{2,1,0:T(8,128)S(1)} %mul.171, f32[3,64,64,64]{3,2,1,0:T(8,128)} %multiply_multiply_fusion), kind=kLoop, calls=%fused_computation.92 | loop fusion | flops 16515072 | bytes 13631488 | tf_op jit(solution)/shard_map/while/body/eval_jaxpr/vmap()/add | solution.py:107
  236.6 15.6 %fusion.56 = f32[1,64,64,64]{3,2,1,0:T(8,128)} fusion(f32[1,64,64,64]{3,2,1,0:T(8,128)} %slice.290), kind=kLoop, calls=%fused_computation.116 | loop fusion | flops 4194304 | bytes 2097152 | tf_op jit(solution)/shard_map/mul | solution.py:184
  254.8 5.1 all-to-all-start.1
  259.9 35.4 %multiply_add_fusion = (f32[3,64,64,64]{3,2,1,0:T(8,128)}, f32[3,64,64,64]{3,2,1,0:T(8,128)}) fusion(f32[3,64,64,64]{3,2,1,0:T(8,128)} %get-tuple-element.101, f32[3,64,64,64]{3,2,1,0:T(8,128)} %get-tuple-element.102), kind=kLoop, calls=%fused_computation.91 | loop fusion | flops 14942208 | bytes 12582912 | tf_op jit(solution)/shard_map/while/body/eval_jaxpr/vmap()/add | solution.py:107
  295.3 42.7 %multiply_reduce_fusion = (f32[64,64,64]{2,1,0:T(8,128)}, f32[3,64,64,64]{3,2,1,0:T(8,128)}) fusion(f32[3,64,64,64]{3,2,1,0:T(8,128)} %get-tuple-element.30, f32[3,64,64,64]{3,2,1,0:T(8,128)} %get-tuple-element.100, f32[3,64,64,64]{3,2,1,0:T(8,128)} %get-tuple-element.99, f32[3,64,64,64]{3,2,1,0:T(8,128)} %get-tuple-element.101, f32[64,64,64]{2,1,0:T(8,128)S(1)} %mul.171), kind=kLoop, calls=%fused_computation.90 | loop fusion | flops 20185088 | bytes 17825792 | tf_op jit(solution)/shard_map/while/body/eval_jaxpr/reduce_sum | solution.py:127
  338.0 6.8 %broadcast_multiply_fusion = f32[3,64,64,64]{3,2,1,0:T(8,128)} fusion(f32[3,64,64,64]{3,2,1,0:T(8,128)} %get-tuple-element.98, f32[64,64,64]{2,1,0:T(8,128)S(1)} %mul.171), kind=kLoop, calls=%fused_computation.95 | loop fusion | flops 786432 | bytes 7340032 | tf_op jit(solution)/shard_map/while/body/eval_jaxpr/vmap()/mul | solution.py:124
  344.7 10.5 %pad.55 = f32[3,96,96,96]{3,2,1,0:T(8,128)} pad(f32[3,64,64,64]{3,2,1,0:T(8,128)} %broadcast_multiply_fusion, f32[]{:T(128)} %constant.49.clone.1), padding=0_0x16_16x16_16x16_16 | pad | bytes 13762564 | tf_op jit(solution)/shard_map/while/body/eval_jaxpr/vmap(jit(_pad))/pad | solution.py:114
  355.2 3.4 broadcast.154
  358.6 20.2 %while.3 = (s32[]{:T(128)}, f32[3,96,96,96]{3,2,1,0:T(8,128)}, s32[3,4]{1,0:T(4,128)S(1)}, f32[3,64,64,64]{3,2,1,0:T(8,128)}, s32[]{:T(128)}) while((s32[]{:T(128)}, f32[3,96,96,96]{3,2,1,0:T(8,128)}, s32[3,4]{1,0:T(4,128)S(1)}, f32[3,64,64,64]{3,2,1,0:T(8,128)}, s32[]{:T(128)}) %tuple.73), condition=%wide.while_cond.1, body=%wide.while_body.1.sunk | while | flops 2 | bytes 4196993 | solution.py:116
  359.2 6.1 %dynamic-slice_dynamic-update-slice_fusion.5 = f32[3,64,64,64]{3,2,1,0:T(8,128)} fusion(f32[3,64,64,64]{3,2,1,0:T(8,128)} %get-tuple-element.218, s32[]{:T(128)} %get-tuple-element.215, f32[3,96,96,96]{3,2,1,0:T(8,128)} %get-tuple-element.221, s32[]{:T(128)} %bitcast.108, s32[]{:T(128)} %bitcast.109, s32[]{:T(128)} %bitcast.110, s32[]{:T(128)} %bitcast.111), kind=kLoop, calls=%fused_computation.4.clone.1 | loop fusion | bytes 4196864 | tf_op jit(solution)/shard_map/while/body/eval_jaxpr/vmap()/gather
  366.0 6.1 %dynamic-slice_dynamic-update-slice_fusion.5 = f32[3,64,64,64]{3,2,1,0:T(8,128)} fusion(f32[3,64,64,64]{3,2,1,0:T(8,128)} %get-tuple-element.218, s32[]{:T(128)} %get-tuple-element.215, f32[3,96,96,96]{3,2,1,0:T(8,128)} %get-tuple-element.221, s32[]{:T(128)} %bitcast.108, s32[]{:T(128)} %bitcast.109, s32[]{:T(128)} %bitcast.110, s32[]{:T(128)} %bitcast.111), kind=kLoop, calls=%fused_computation.4.clone.1 | loop fusion | bytes 4196864 | tf_op jit(solution)/shard_map/while/body/eval_jaxpr/vmap()/gather
  372.7 6.1 %dynamic-slice_dynamic-update-slice_fusion.5 = f32[3,64,64,64]{3,2,1,0:T(8,128)} fusion(f32[3,64,64,64]{3,2,1,0:T(8,128)} %get-tuple-element.218, s32[]{:T(128)} %get-tuple-element.215, f32[3,96,96,96]{3,2,1,0:T(8,128)} %get-tuple-element.221, s32[]{:T(128)} %bitcast.108, s32[]{:T(128)} %bitcast.109, s32[]{:T(128)} %bitcast.110, s32[]{:T(128)} %bitcast.111), kind=kLoop, calls=%fused_computation.4.clone.1 | loop fusion | bytes 4196864 | tf_op jit(solution)/shard_map/while/body/eval_jaxpr/vmap()/gather
  378.8 5.3 broadcast_in_dim.31
  384.1 11.9 %scatter_fusion = f32[5,64,64,64]{3,2,1,0:T(8,128)} fusion(f32[5,64,64,64]{3,2,1,0:T(8,128)} %broadcast_in_dim.31, s32[3]{0:T(128)S(1)} %fusion.77, f32[3,64,64,64]{3,2,1,0:T(8,128)} %get-tuple-element.38), kind=kCustom, calls=%fused_computation.1 | custom fusion | flops 786432 | bytes 9437196 | tf_op jit(solution)/shard_map/scatter-add | solution.py:182
  396.1 8.4 %slice.400 = f32[4,64,64,64]{3,2,1,0:T(8,128)} slice(f32[5,64,64,64]{3,2,1,0:T(8,128)} %scatter_fusion), slice={[1:5], [0:64], [0:64], [0:64]} | slice | bytes 8388608 | tf_op jit(solution)/shard_map/slice | solution.py:185
  404.5 7.4 %concatenate.27 = f32[4,64,32,128]{3,2,1,0:T(8,128)} reshape(f32[4,64,64,64]{3,2,1,0:T(8,128)} %slice.400) | data formatting | bytes 8388608 | tf_op jit(solution)/shard_map/concatenate | solution.py:185
  422.8 4.6 all_to_all.35
  427.4 9.7 %all-to-all-start.3 = ((f32[32,2,5,32,128]{4,3,1,2,0:T(8,128)}), f32[32,2,5,32,128]{4,3,1,2,0:T(8,128)}, u32[]{:S(2)}, u32[]{:S(2)}) async-start(f32[32,2,5,32,128]{4,3,1,2,0:T(8,128)} %copy.75), calls=%async_computation.3 | async-start | bytes 10485760 | tf_op jit(solution)/shard_map/all_to_all | solution.py:40
  437.2 120.5 %all-to-all-done.3 = f32[32,2,5,32,128]{4,3,1,2,0:T(8,128)} async-done(((f32[32,2,5,32,128]{4,3,1,2,0:T(8,128)}), f32[32,2,5,32,128]{4,3,1,2,0:T(8,128)}, u32[]{:S(2)}, u32[]{:S(2)}) %all-to-all-start.3) | async-done | bytes 5242912 | tf_op jit(solution)/shard_map/all_to_all | solution.py:40
  560.9 7.9 %all_to_all.36 = f32[32,2,5,32,128]{4,3,0,2,1:T(8,128)S(1)} all-to-all(f32[32,2,5,32,128]{4,3,0,2,1:T(8,128)S(1)} %copy.76), channel_id=1, replica_groups=mesh['orb'=4,'grid_0'=8,'grid_1'=4,'grid_2'=2] {'grid_2'}, dimensions={1} | all-to-all | bytes 10485760 | tf_op jit(solution)/shard_map/all_to_all | solution.py:40
  571.5 4.5 collective-permute-done.1
  (64 shorter events, 38.0 us)
Async XLA Ops:
  1.5 5.6 collective-permute-start
  7.3 14.6 %copy-start.5 = (s32[1,3,3]{2,0,1:T(1,128)S(1)}, s32[1,3,3]{2,0,1:T(1,128)}, u32[]{:S(2)}) copy-start(s32[1,3,3]{2,0,1:T(1,128)} %param.9) | copy-start | bytes 112
  7.4 15.0 %copy-start.6 = (s32[1,3]{1,0:T(1,128)S(1)}, s32[1,3]{1,0:T(1,128)}, u32[]{:S(2)}) copy-start(s32[1,3]{1,0:T(1,128)} %param.8) | copy-start | bytes 40
  7.4 2.3 copy-start.2
  9.8 130.8 %all-to-all-start = ((f32[320,32,128]{2,1,0:T(8,128)}), f32[320,32,128]{2,1,0:T(8,128)}, u32[]{:S(2)}, u32[]{:S(2)}) async-start(f32[320,32,128]{2,1,0:T(8,128)} %bitcast.114), calls=%async_computation | async-start | bytes 10485760 | tf_op jit(solution)/shard_map/all_to_all | solution.py:167
  254.8 167.9 %all-to-all-start.1 = ((f32[32,2,1,32,128]{4,3,1,2,0:T(8,128)}), f32[32,2,1,32,128]{4,3,1,2,0:T(8,128)S(1)}, u32[]{:S(2)}, u32[]{:S(2)}) async-start(f32[32,2,1,32,128]{4,3,1,2,0:T(8,128)} %reshape_transpose_reshape_reshape.3), calls=%async_computation.1 | async-start | bytes 2097152 | tf_op jit(solution)/shard_map/all_to_all | solution.py:40
  404.5 7.4 %copy-start.1 = (f32[64,64,64]{2,1,0:T(8,128)S(1)}, f32[64,64,64]{2,1,0:T(8,128)}, u32[]{:S(2)}) copy-start(f32[64,64,64]{2,1,0:T(8,128)} %get-tuple-element.97) | copy-start | bytes 3145732
  427.4 130.4 %all-to-all-start.3 = ((f32[32,2,5,32,128]{4,3,1,2,0:T(8,128)}), f32[32,2,5,32,128]{4,3,1,2,0:T(8,128)}, u32[]{:S(2)}, u32[]{:S(2)}) async-start(f32[32,2,5,32,128]{4,3,1,2,0:T(8,128)} %copy.75), calls=%async_computation.3 | async-start | bytes 10485760 | tf_op jit(solution)/shard_map/all_to_all | solution.py:40
  570.5 5.6 copy-start
  570.5 5.6 copy-start.3
  570.5 5.6 copy-start.4
  570.5 5.6 collective-permute-start.1
where the time goes:
time: 580 us; the launch traced here: 578 us
  waiting for transfers between devices  243 us (42%)
  other arithmetic  163 us (28%)
  local copies, waits for them, and re-layouts  128 us (22%)
  starting transfers between devices  30.4 us (5%)
  blocking collectives  12.5 us (2%)
    all_to_all x2, waiting for transfers between devices, exchange_in_order(): out = lax.all_to_all(out, axes[k], k, k, tiled=True)  121 us
    all_to_all x1, waiting for transfers between devices, local(): lax.all_to_all(windows, GRID, split_axis=0, concat_axis=1, tiled=True)  118 us
    add x2, other arithmetic, solve_potential(): direction = keep_weight * direction + residual_weight * residual  70.7 us
    reduce_sum x1, other arithmetic, pair_terms(): return (jnp.sum(own_terms, axis=0), partner_terms)  42.7 us
    gather x18, local copies, waits for them, and re-layouts  40.7 us
    pad x2, local copies, waits for them, and re-layouts, shift_box(): padded = jnp.pad(one_box, reach_cells)  21 us
    mul x1, other arithmetic, local(): -0.5 * apply_operator(own_boxes)  15.6 us
    all_to_all x2, starting transfers between devices, exchange_in_order(): out = lax.all_to_all(out, axes[k], k, k, tiled=True)  14.8 us
  transfers between devices with their start and end apart: 5, of which 3 were waited for; matrix products, arithmetic and copies ran while one was open for 29% of the time, Pallas kernels for 0%

commit v1 on v0

--- a/solution.py
+++ b/solution.py
@@ -164,7 +164,10 @@
     steps_ahead = -(-AHEAD // count_local)
     upper_rows = from_behind(orbitals[:AHEAD], "orb", -1)
     windows = build_windows(orbitals, upper_rows, count_local, steps_ahead)
-    widened = lax.all_to_all(windows, GRID, split_axis=0, concat_axis=1, tiled=True)
+    widened = jnp.concatenate(
+        lax.all_to_all(jnp.stack(jnp.split(windows, lax.axis_size(GRID), axis=0)), GRID, 0, 0),
+        axis=1,
+    )
     full_rows = widened.shape[1]
     extended = widened.reshape(count_local + AHEAD, B, B, B)
     own_boxes = extended[:count_local]

time: 580 us -> 583 us (level)
    another operation x0 -> x1, local copies, waits for them, and re-layouts: none -> 8.53 us  [local(): extended = widened.reshape(count_local + AHEAD, B, B, B)]
    reshape x1 -> x0, local copies, waits for them, and re-layouts: 8.52 us -> none  [local(): extended = widened.reshape(count_local + AHEAD, B, B, B)]
    unnamed x25 -> x23, local copies, waits for them, and re-layouts: 13 us -> 14.9 us
where the time goes in v1:
time: 583 us; the launch traced here: 581 us
  waiting for transfers between devices  243 us (42%)
  other arithmetic  163 us (28%)
  local copies, waits for them, and re-layouts  131 us (22%)
  starting transfers between devices  30.1 us (5%)
  blocking collectives  12.5 us (2%)
    all_to_all x2, waiting for transfers between devices, exchange_in_order(): out = lax.all_to_all(out, axes[k], k, k, tiled=True)  121 us
    all_to_all x1, waiting for transfers between devices, local(): lax.all_to_all(jnp.stack(jnp.split(windows, lax.axis_size(GRID), axis=0))...  118 us
    add x2, other arithmetic, solve_potential(): direction = keep_weight * direction + residual_weight * residual  70.9 us
    reduce_sum x1, other arithmetic, pair_terms(): return (jnp.sum(own_terms, axis=0), partner_terms)  42.6 us
    gather x18, local copies, waits for them, and re-layouts  40.7 us
    pad x2, local copies, waits for them, and re-layouts, shift_box(): padded = jnp.pad(one_box, reach_cells)  21 us
    mul x1, other arithmetic, local(): -0.5 * apply_operator(own_boxes)  15.6 us
    unnamed x23, local copies, waits for them, and re-layouts  14.9 us
  transfers between devices with their start and end apart: 5, of which 3 were waited for; matrix products, arithmetic and copies ran while one was open for 29% of the time, Pallas kernels for 0%

profile of v1, /device:TPU:2, one launch (start us, length us, event | category | flops | bytes accessed | tf_op | source)
XLA Modules:
  0.0 580.9 jit_solution(7266696677688296137)
XLA Ops:
  12.6 12.2 %all-to-all-start = ((f32[64,5,32,128]{3,2,1,0:T(8,128)}), f32[64,5,32,128]{3,2,1,0:T(8,128)}, u32[]{:S(2)}, u32[]{:S(2)}) async-start(f32[64,5,32,128]{3,2,1,0:T(8,128)} %fusion.64), calls=%async_computation | async-start | bytes 10485760 | tf_op jit(solution)/shard_map/all_to_all | solution.py:168
  25.2 118.1 %all-to-all-done = f32[64,5,32,128]{3,2,1,0:T(8,128)} async-done(((f32[64,5,32,128]{3,2,1,0:T(8,128)}), f32[64,5,32,128]{3,2,1,0:T(8,128)}, u32[]{:S(2)}, u32[]{:S(2)}) %all-to-all-start) | async-done | bytes 5242912 | tf_op jit(solution)/shard_map/all_to_all | solution.py:168
  143.4 8.5 %reshape_reshape.8 = f32[5,64,64,64]{3,2,0,1:T(8,128)} reshape(f32[5,64,32,128]{3,2,0,1:T(8,128)} %bitcast.8) | data formatting | bytes 10485760 | tf_op jit(solution)/shard_map/reshape;reshape | solution.py:172
  155.3 7.5 %gather_fusion = f32[3,64,64,64]{3,2,1,0:T(8,128)} fusion(f32[5,64,64,64]{3,2,0,1:T(8,128)} %reshape_reshape.8, s32[1024]{0:T(1024)S(1)} %pad_clamp_fusion), kind=kCustom, calls=%fused_computation | custom fusion | bytes 6291468 | tf_op jit(solution)/shard_map/while/body/eval_jaxpr/gather | solution.py:179
  162.8 10.5 %pad.51 = f32[3,96,96,96]{3,2,1,0:T(8,128)} pad(f32[3,64,64,64]{3,2,1,0:T(8,128)} %gather_fusion, f32[]{:T(128)} %constant.49.clone.1), padding=0_0x16_16x16_16x16_16 | pad | bytes 13762564 | tf_op jit(solution)/shard_map/while/body/eval_jaxpr/vmap(jit(_pad))/pad | solution.py:114
  173.3 3.5 broadcast.154.clone
  176.8 20.5 %while.2 = (s32[]{:T(128)}, f32[3,96,96,96]{3,2,1,0:T(8,128)}, s32[3,4]{1,0:T(4,128)S(1)}, f32[3,64,64,64]{3,2,1,0:T(8,128)}, s32[]{:T(128)}) while((s32[]{:T(128)}, f32[3,96,96,96]{3,2,1,0:T(8,128)}, s32[3,4]{1,0:T(4,128)S(1)}, f32[3,64,64,64]{3,2,1,0:T(8,128)}, s32[]{:T(128)}) %tuple.68), condition=%wide.while_cond, body=%wide.while_body.sunk | while | flops 2 | bytes 4196993 | solution.py:116
  177.4 6.2 %dynamic-slice_dynamic-update-slice_fusion.4 = f32[3,64,64,64]{3,2,1,0:T(8,128)} fusion(f32[3,64,64,64]{3,2,1,0:T(8,128)} %get-tuple-element.195, s32[]{:T(128)} %get-tuple-element.192, f32[3,96,96,96]{3,2,1,0:T(8,128)} %get-tuple-element.198, s32[]{:T(128)} %bitcast.101, s32[]{:T(128)} %bitcast.102, s32[]{:T(128)} %bitcast.103, s32[]{:T(128)} %bitcast.104), kind=kLoop, calls=%fused_computation.2.clone.1 | loop fusion | bytes 4196864 | tf_op jit(solution)/shard_map/while/body/eval_jaxpr/vmap()/gather
  184.3 6.1 %dynamic-slice_dynamic-update-slice_fusion.4 = f32[3,64,64,64]{3,2,1,0:T(8,128)} fusion(f32[3,64,64,64]{3,2,1,0:T(8,128)} %get-tuple-element.195, s32[]{:T(128)} %get-tuple-element.192, f32[3,96,96,96]{3,2,1,0:T(8,128)} %get-tuple-element.198, s32[]{:T(128)} %bitcast.101, s32[]{:T(128)} %bitcast.102, s32[]{:T(128)} %bitcast.103, s32[]{:T(128)} %bitcast.104), kind=kLoop, calls=%fused_computation.2.clone.1 | loop fusion | bytes 4196864 | tf_op jit(solution)/shard_map/while/body/eval_jaxpr/vmap()/gather
  191.1 6.2 %dynamic-slice_dynamic-update-slice_fusion.4 = f32[3,64,64,64]{3,2,1,0:T(8,128)} fusion(f32[3,64,64,64]{3,2,1,0:T(8,128)} %get-tuple-element.195, s32[]{:T(128)} %get-tuple-element.192, f32[3,96,96,96]{3,2,1,0:T(8,128)} %get-tuple-element.198, s32[]{:T(128)} %bitcast.101, s32[]{:T(128)} %bitcast.102, s32[]{:T(128)} %bitcast.103, s32[]{:T(128)} %bitcast.104), kind=kLoop, calls=%fused_computation.2.clone.1 | loop fusion | bytes 4196864 | tf_op jit(solution)/shard_map/while/body/eval_jaxpr/vmap()/gather
  197.2 6.9 %multiply_multiply_fusion = f32[3,64,64,64]{3,2,1,0:T(8,128)} fusion(f32[3,64,64,64]{3,2,1,0:T(8,128)} %get-tuple-element.30, f32[64,64,64]{2,1,0:T(8,128)S(1)} %mul.171), kind=kLoop, calls=%fused_computation.93 | loop fusion | flops 1572864 | bytes 7340032 | tf_op jit(solution)/shard_map/while/body/eval_jaxpr/vmap()/div | solution.py:100
  204.1 35.3 %multiply_add_fusion.1 = (f32[3,64,64,64]{3,2,1,0:T(8,128)}, f32[3,64,64,64]{3,2,1,0:T(8,128)}) fusion(f32[3,64,64,64]{3,2,1,0:T(8,128)} %get-tuple-element.30, f32[64,64,64]{2,1,0:T(8,128)S(1)} %mul.171, f32[3,64,64,64]{3,2,1,0:T(8,128)} %multiply_multiply_fusion), kind=kLoop, calls=%fused_computation.92 | loop fusion | flops 16515072 | bytes 13631488 | tf_op jit(solution)/shard_map/while/body/eval_jaxpr/vmap()/add | solution.py:107
  239.4 15.6 %fusion.56 = f32[1,64,64,64]{3,2,1,0:T(8,128)} fusion(f32[1,64,64,64]{3,2,1,0:T(8,128)} %slice.355), kind=kLoop, calls=%fused_computation.116 | loop fusion | flops 4194304 | bytes 2097152 | tf_op jit(solution)/shard_map/mul | solution.py:187
  257.6 5.1 all-to-all-start.1
  262.6 35.6 %multiply_add_fusion = (f32[3,64,64,64]{3,2,1,0:T(8,128)}, f32[3,64,64,64]{3,2,1,0:T(8,128)}) fusion(f32[3,64,64,64]{3,2,1,0:T(8,128)} %get-tuple-element.93, f32[3,64,64,64]{3,2,1,0:T(8,128)} %get-tuple-element.94), kind=kLoop, calls=%fused_computation.91 | loop fusion | flops 14942208 | bytes 12582912 | tf_op jit(solution)/shard_map/while/body/eval_jaxpr/vmap()/add | solution.py:107
  298.3 42.6 %multiply_reduce_fusion = (f32[64,64,64]{2,1,0:T(8,128)}, f32[3,64,64,64]{3,2,1,0:T(8,128)}) fusion(f32[3,64,64,64]{3,2,1,0:T(8,128)} %get-tuple-element.30, f32[3,64,64,64]{3,2,1,0:T(8,128)} %get-tuple-element.92, f32[3,64,64,64]{3,2,1,0:T(8,128)} %get-tuple-element.91, f32[3,64,64,64]{3,2,1,0:T(8,128)} %get-tuple-element.93, f32[64,64,64]{2,1,0:T(8,128)S(1)} %mul.171), kind=kLoop, calls=%fused_computation.90 | loop fusion | flops 20185088 | bytes 17825792 | tf_op jit(solution)/shard_map/while/body/eval_jaxpr/reduce_sum | solution.py:127
  340.9 6.8 %broadcast_multiply_fusion = f32[3,64,64,64]{3,2,1,0:T(8,128)} fusion(f32[3,64,64,64]{3,2,1,0:T(8,128)} %get-tuple-element.90, f32[64,64,64]{2,1,0:T(8,128)S(1)} %mul.171), kind=kLoop, calls=%fused_computation.95 | loop fusion | flops 786432 | bytes 7340032 | tf_op jit(solution)/shard_map/while/body/eval_jaxpr/vmap()/mul | solution.py:124
  347.6 10.5 %pad.55 = f32[3,96,96,96]{3,2,1,0:T(8,128)} pad(f32[3,64,64,64]{3,2,1,0:T(8,128)} %broadcast_multiply_fusion, f32[]{:T(128)} %constant.49.clone.1), padding=0_0x16_16x16_16x16_16 | pad | bytes 13762564 | tf_op jit(solution)/shard_map/while/body/eval_jaxpr/vmap(jit(_pad))/pad | solution.py:114
  358.1 3.4 broadcast.154
  361.5 20.2 %while.3 = (s32[]{:T(128)}, f32[3,96,96,96]{3,2,1,0:T(8,128)}, s32[3,4]{1,0:T(4,128)S(1)}, f32[3,64,64,64]{3,2,1,0:T(8,128)}, s32[]{:T(128)}) while((s32[]{:T(128)}, f32[3,96,96,96]{3,2,1,0:T(8,128)}, s32[3,4]{1,0:T(4,128)S(1)}, f32[3,64,64,64]{3,2,1,0:T(8,128)}, s32[]{:T(128)}) %tuple.71), condition=%wide.while_cond.1, body=%wide.while_body.1.sunk | while | flops 2 | bytes 4196993 | solution.py:116
  362.1 6.1 %dynamic-slice_dynamic-update-slice_fusion.5 = f32[3,64,64,64]{3,2,1,0:T(8,128)} fusion(f32[3,64,64,64]{3,2,1,0:T(8,128)} %get-tuple-element.210, s32[]{:T(128)} %get-tuple-element.207, f32[3,96,96,96]{3,2,1,0:T(8,128)} %get-tuple-element.213, s32[]{:T(128)} %bitcast.105, s32[]{:T(128)} %bitcast.106, s32[]{:T(128)} %bitcast.107, s32[]{:T(128)} %bitcast.108), kind=kLoop, calls=%fused_computation.4.clone.1 | loop fusion | bytes 4196864 | tf_op jit(solution)/shard_map/while/body/eval_jaxpr/vmap()/gather
  368.9 6.1 %dynamic-slice_dynamic-update-slice_fusion.5 = f32[3,64,64,64]{3,2,1,0:T(8,128)} fusion(f32[3,64,64,64]{3,2,1,0:T(8,128)} %get-tuple-element.210, s32[]{:T(128)} %get-tuple-element.207, f32[3,96,96,96]{3,2,1,0:T(8,128)} %get-tuple-element.213, s32[]{:T(128)} %bitcast.105, s32[]{:T(128)} %bitcast.106, s32[]{:T(128)} %bitcast.107, s32[]{:T(128)} %bitcast.108), kind=kLoop, calls=%fused_computation.4.clone.1 | loop fusion | bytes 4196864 | tf_op jit(solution)/shard_map/while/body/eval_jaxpr/vmap()/gather
  375.7 6.1 %dynamic-slice_dynamic-update-slice_fusion.5 = f32[3,64,64,64]{3,2,1,0:T(8,128)} fusion(f32[3,64,64,64]{3,2,1,0:T(8,128)} %get-tuple-element.210, s32[]{:T(128)} %get-tuple-element.207, f32[3,96,96,96]{3,2,1,0:T(8,128)} %get-tuple-element.213, s32[]{:T(128)} %bitcast.105, s32[]{:T(128)} %bitcast.106, s32[]{:T(128)} %bitcast.107, s32[]{:T(128)} %bitcast.108), kind=kLoop, calls=%fused_computation.4.clone.1 | loop fusion | bytes 4196864 | tf_op jit(solution)/shard_map/while/body/eval_jaxpr/vmap()/gather
  381.7 5.3 broadcast_in_dim.31
  387.1 11.9 %scatter_fusion = f32[5,64,64,64]{3,2,1,0:T(8,128)} fusion(f32[5,64,64,64]{3,2,1,0:T(8,128)} %broadcast_in_dim.31, s32[3]{0:T(128)S(1)} %fusion.77, f32[3,64,64,64]{3,2,1,0:T(8,128)} %get-tuple-element.38), kind=kCustom, calls=%fused_computation.1 | custom fusion | flops 786432 | bytes 9437196 | tf_op jit(solution)/shard_map/scatter-add | solution.py:185
  399.0 8.4 %slice.465 = f32[4,64,64,64]{3,2,1,0:T(8,128)} slice(f32[5,64,64,64]{3,2,1,0:T(8,128)} %scatter_fusion), slice={[1:5], [0:64], [0:64], [0:64]} | slice | bytes 8388608 | tf_op jit(solution)/shard_map/slice | solution.py:188
  407.4 7.4 %concatenate.27 = f32[4,64,32,128]{3,2,1,0:T(8,128)} reshape(f32[4,64,64,64]{3,2,1,0:T(8,128)} %slice.465) | data formatting | bytes 8388608 | tf_op jit(solution)/shard_map/concatenate | solution.py:188
  425.8 4.6 all_to_all.25
  430.4 9.8 %all-to-all-start.3 = ((f32[32,2,5,32,128]{4,3,1,2,0:T(8,128)}), f32[32,2,5,32,128]{4,3,1,2,0:T(8,128)}, u32[]{:S(2)}, u32[]{:S(2)}) async-start(f32[32,2,5,32,128]{4,3,1,2,0:T(8,128)} %copy.64), calls=%async_computation.3 | async-start | bytes 10485760 | tf_op jit(solution)/shard_map/all_to_all | solution.py:40
  440.2 120.5 %all-to-all-done.3 = f32[32,2,5,32,128]{4,3,1,2,0:T(8,128)} async-done(((f32[32,2,5,32,128]{4,3,1,2,0:T(8,128)}), f32[32,2,5,32,128]{4,3,1,2,0:T(8,128)}, u32[]{:S(2)}, u32[]{:S(2)}) %all-to-all-start.3) | async-done | bytes 5242912 | tf_op jit(solution)/shard_map/all_to_all | solution.py:40
  563.9 7.9 %all_to_all.26 = f32[32,2,5,32,128]{4,3,0,2,1:T(8,128)S(1)} all-to-all(f32[32,2,5,32,128]{4,3,0,2,1:T(8,128)S(1)} %copy.65), channel_id=1, replica_groups=mesh['orb'=4,'grid_0'=8,'grid_1'=4,'grid_2'=2] {'grid_2'}, dimensions={1} | all-to-all | bytes 10485760 | tf_op jit(solution)/shard_map/all_to_all | solution.py:40
  574.3 4.8 collective-permute-done.1
  (62 shorter events, 40.5 us)
Async XLA Ops:
  1.5 6.7 %collective-permute-start = (f32[4,32,128]{2,1,0:T(8,128)S(1)}, f32[4,32,128]{2,1,0:T(8,128)S(1)}, u32[]{:S(2)}, u32[]{:S(2)}) collective-permute-start(f32[4,32,128]{2,1,0:T(8,128)S(1)} %slice.345), channel_id=1, source_target_pairs={{0,192},{64,0},{128,64},{192,128},{1,193},{65,1},{129,65},{193,129... | collective-permute-start | bytes 196616 | tf_op jit(solution)/shard_map/ppermute | solution.py:22
  11.5 13.3 %copy-start.4 = (s32[1,3,3]{2,0,1:T(1,128)S(1)}, s32[1,3,3]{2,0,1:T(1,128)}, u32[]{:S(2)}) copy-start(s32[1,3,3]{2,0,1:T(1,128)} %param.9) | copy-start | bytes 112
  11.5 13.7 %copy-start.5 = (s32[1,3]{1,0:T(1,128)S(1)}, s32[1,3]{1,0:T(1,128)}, u32[]{:S(2)}) copy-start(s32[1,3]{1,0:T(1,128)} %param.8) | copy-start | bytes 40
  12.6 130.8 %all-to-all-start = ((f32[64,5,32,128]{3,2,1,0:T(8,128)}), f32[64,5,32,128]{3,2,1,0:T(8,128)}, u32[]{:S(2)}, u32[]{:S(2)}) async-start(f32[64,5,32,128]{3,2,1,0:T(8,128)} %fusion.64), calls=%async_computation | async-start | bytes 10485760 | tf_op jit(solution)/shard_map/all_to_all | solution.py:168
  257.6 168.2 %all-to-all-start.1 = ((f32[32,2,1,32,128]{4,3,1,2,0:T(8,128)}), f32[32,2,1,32,128]{4,3,1,2,0:T(8,128)S(1)}, u32[]{:S(2)}, u32[]{:S(2)}) async-start(f32[32,2,1,32,128]{4,3,1,2,0:T(8,128)} %reshape_transpose_reshape_reshape.3), calls=%async_computation.1 | async-start | bytes 2097152 | tf_op jit(solution)/shard_map/all_to_all | solution.py:40
  407.4 7.4 %copy-start.1 = (f32[64,64,64]{2,1,0:T(8,128)S(1)}, f32[64,64,64]{2,1,0:T(8,128)}, u32[]{:S(2)}) copy-start(f32[64,64,64]{2,1,0:T(8,128)} %get-tuple-element.89) | copy-start | bytes 3145732
  430.4 130.4 %all-to-all-start.3 = ((f32[32,2,5,32,128]{4,3,1,2,0:T(8,128)}), f32[32,2,5,32,128]{4,3,1,2,0:T(8,128)}, u32[]{:S(2)}, u32[]{:S(2)}) async-start(f32[32,2,5,32,128]{4,3,1,2,0:T(8,128)} %copy.64), calls=%async_computation.3 | async-start | bytes 10485760 | tf_op jit(solution)/shard_map/all_to_all | solution.py:40
  573.5 5.6 copy-start
  573.5 5.6 copy-start.2
  573.5 5.6 copy-start.3
  573.5 5.6 collective-permute-start.1
